TPU v7x, 256 devices: a whole 4x4x8 slice. The times are simulated.
256 devices in a mesh: dp: 32 (over x, y, z_hi), mp: 8 (over z_lo, core).
Axes of the slice: x: 4, y: 4, z: 8 (z_hi: 2, z_lo: 4; z = z_hi * 4 + z_lo), core: 2. Of those that a mesh axis runs over, the one named last changes fastest.
Arguments:
- tokens: bfloat16 [1024, 7168], P('dp', 'mp'), may hold values from -6 to 6
- gate_weight: bfloat16 [7168, 18432], P('mp', 'dp'), may hold values from -0.0625 to 0.0625
- up_weight: bfloat16 [7168, 18432], P('mp', 'dp'), may hold values from -0.0625 to 0.0625
- down_weight: bfloat16 [18432, 7168], P('dp', 'mp'), may hold values from -0.046875 to 0.046875
- gate_round: bfloat16 [7168, 18432], P('mp', 'dp'), may hold values from -8 to 8
- up_round: bfloat16 [7168, 18432], P('mp', 'dp'), may hold values from -8 to 8
- down_round: bfloat16 [18432, 7168], P('dp', 'mp'), may hold values from -8 to 8
- quant_scale: float32 [2, 18432], P(None, 'dp'), may hold values from 0.3 to 3
- quant_bits: int32 [2, 18432], P(None, 'dp'), may hold values from 2 to 4
- quant_zero: int32 [2, 18432], P(None, 'dp'), may hold values from 0 to 2
- down_scale: float32 [7168], P('mp'), may hold values from 0.3 to 3
- down_bits: int32 [7168], P('mp'), may hold values from 2 to 4
- down_zero: int32 [7168], P('mp'), may hold values from 0 to 2
- fisher: float32 [1024], replicated, may hold values from 1 to 300, as said below
Outputs:
- loss_value: float32 [], replicated
- grad_gate: bfloat16 [7168, 18432], P('mp', 'dp')
- grad_up: bfloat16 [7168, 18432], P('mp', 'dp')
- grad_down: bfloat16 [18432, 7168], P('dp', 'mp')
Inputs may be any that keep to these rules, and one draw needn't show every extreme that they name: `fisher`: positive weights.
All inputs are finite; a program needn't handle non-finite values.
Results may differ from a plain program's by a relative error of at most 0.0059.
Values may be sent and summed in bfloat16 or wider, within the bound.
No kernel may reach another device: no remote copies, remote signals or barrier semaphores. Data moves between devices by JAX's collectives and lax.ppermute only.
A program may use at most 128 MiB of HBM per device.

v0:
```python
import jax
import jax.numpy as jnp
from jax import lax
from jax.sharding import Mesh
from jax.sharding import PartitionSpec as P

D = 7168
FF = 18432
DP = ("dp_0", "dp_1", "dp_2")
MP = ("mp_0", "mp_1")
DP_MP = ("dp_0", "dp_1", "dp_2", "mp_0", "mp_1")


def in_order(tiles, dim):
    tiles = jnp.moveaxis(tiles, 0, dim)
    shape = tiles.shape
    return tiles.reshape(*shape[:dim], shape[dim] * shape[dim + 1], *shape[dim + 2 :])


def copy_for_each(value, axis):
    copies = jnp.broadcast_to(value, (lax.axis_size(axis), *value.shape))
    return lax.all_to_all(copies, axis, split_axis=0, concat_axis=0, tiled=True)


def gathered_copies(value, axis, dim):
    return in_order(copy_for_each(value, axis), dim)


def scatter_axes(value, axes, dim):
    if not axes:
        return value
    nearer = lax.psum_scatter(value, axes[0], scatter_dimension=dim, tiled=True)
    return scatter_axes(nearer, axes[1:], dim)


def over_axes(value, axes):
    for axis in axes:
        value = lax.psum(value, axis)
    return value


def split_up(value, dim, count):
    shape = value.shape
    tiles = value.reshape(*shape[:dim], count, shape[dim] // count, *shape[dim + 1 :])
    return jnp.moveaxis(tiles, dim, 0)


def sent_and_summed(value, axis, dim):
    count = lax.axis_size(axis)
    tiles = lax.all_to_all(split_up(value, dim, count), axis, 0, 0, tiled=True)
    return jnp.sum(tiles, axis=0)


def soft_weight(weight, variable, channel_scale, bit_width, zero_point, fan_in):
    quant_step = channel_scale / jnp.sqrt(jnp.float32(fan_in))
    offset = jnp.clip(1.2 * jax.nn.sigmoid(variable.astype(jnp.float32)) - 0.1, 0.0, 1.0)
    ceiling = (jnp.left_shift(jnp.int32(1), bit_width) - 1).astype(jnp.float32)
    zero_level = zero_point.astype(jnp.float32)
    levels = jnp.clip(
        weight.astype(jnp.float32) / quant_step + offset - 0.5 + zero_level, 0.0, ceiling
    )
    return (quant_step * (levels - zero_level)).astype(jnp.bfloat16)


def contract_rows(left, right):
    return lax.dot_general(
        left, right, (((0,), (0,)), ((), ())), preferred_element_type=jnp.float32
    )


def shards(
    tokens,
    gate_weight,
    up_weight,
    down_weight,
    gate_round,
    up_round,
    down_round,
    quant_scale,
    quant_bits,
    quant_zero,
    down_scale,
    down_bits,
    down_zero,
    fisher,
):
    own_rows = tokens.shape[0]
    hidden_cols = gate_weight.shape[1]
    all_tokens = lax.all_gather(tokens, DP, axis=0, tiled=True)
    total_rows = all_tokens.shape[0]
    gate_student = soft_weight(
        gate_weight, gate_round, quant_scale[0], quant_bits[0], quant_zero[0], D
    )
    up_student = soft_weight(up_weight, up_round, quant_scale[1], quant_bits[1], quant_zero[1], D)
    stacked = jnp.concatenate([gate_weight, up_weight, gate_student, up_student], axis=1)
    partial_value = jnp.dot(all_tokens, stacked, preferred_element_type=jnp.float32)
    shares = lax.psum_scatter(partial_value, MP, scatter_dimension=0, tiled=True)
    gate_teacher = shares[:, :hidden_cols]
    up_teacher = shares[:, hidden_cols : 2 * hidden_cols]
    gate_own = shares[:, 2 * hidden_cols : 3 * hidden_cols]
    up_own = shares[:, 3 * hidden_cols :]
    hidden_teacher = (jax.nn.silu(gate_teacher) * up_teacher).astype(jnp.bfloat16)
    hidden_student = (jax.nn.silu(gate_own) * up_own).astype(jnp.bfloat16)
    hidden = gathered_copies(jnp.concatenate([hidden_teacher, hidden_student], axis=1), MP, 0)
    down_student = soft_weight(down_weight, down_round, down_scale, down_bits, down_zero, FF)
    terms = jnp.dot(
        hidden,
        jnp.concatenate([-down_weight, down_student], axis=0),
        preferred_element_type=jnp.float32,
    )
    summed = scatter_axes(terms, DP, 0)
    token_weight = lax.dynamic_slice_in_dim(fisher, lax.axis_index(DP) * own_rows, own_rows)
    weighted = token_weight[:, None] * summed
    partial_loss = jnp.sum(weighted * summed)
    local_grad = (2.0 * weighted).astype(jnp.bfloat16)
    loss_sum = over_axes(partial_loss, DP_MP)
    out_grad = lax.all_gather(local_grad, DP, axis=0, tiled=True)
    loss_value = loss_sum / (total_rows * D)
    grad_down = contract_rows(hidden[:, hidden_cols:], out_grad).astype(jnp.bfloat16)
    hidden_part = lax.dot_general(
        out_grad, down_student, (((1,), (1,)), ((), ())), preferred_element_type=jnp.float32
    )
    hidden_grad = sent_and_summed(hidden_part, MP, 0)
    sigmoid_gate = jax.nn.sigmoid(gate_own)
    gate_grad = (
        hidden_grad * up_own * sigmoid_gate * (1.0 + gate_own * (1.0 - sigmoid_gate))
    ).astype(jnp.bfloat16)
    up_grad = (hidden_grad * gate_own * sigmoid_gate).astype(jnp.bfloat16)
    both_grads = gathered_copies(jnp.concatenate([gate_grad, up_grad], axis=1), MP, 0)
    weight_grads = contract_rows(all_tokens, both_grads)
    grad_gate = weight_grads[:, :hidden_cols].astype(jnp.bfloat16)
    grad_up = weight_grads[:, hidden_cols:].astype(jnp.bfloat16)
    return (loss_value, grad_gate, grad_up, grad_down)


def solution(mesh):
    split = Mesh(mesh.devices.reshape(4, 4, 2, 4, 2), ("dp_0", "dp_1", "dp_2", "mp_0", "mp_1"))
    return jax.shard_map(
        shards,
        mesh=split,
        in_specs=(
            P(DP, MP),
            P(MP, DP),
            P(MP, DP),
            P(DP, MP),
            P(MP, DP),
            P(MP, DP),
            P(DP, MP),
            P(None, DP),
            P(None, DP),
            P(None, DP),
            P(MP),
            P(MP),
            P(MP),
            P(),
        ),
        out_specs=(P(), P(MP, DP), P(MP, DP), P(DP, MP)),
        check_vma=False,
    )
```

profile of v0, /device:TPU:65, one launch (start us, length us, event | category | flops | bytes accessed | tf_op | source)
XLA Modules:
  0.0 616.8 jit_solution(13538513241438266588)
XLA Ops:
  10.3 4.8 multiply_convert_fusion.1
  15.1 83.8 %all-gather.3.cloned.1.call-done = bf16[1024,896]{1,0:T(8,128)(2,1)} async-done(((bf16[32,896]{1,0:T(8,128)(2,1)}), bf16[1024,896]{1,0:T(8,128)(2,1)}) %all-gather.3.cloned.1.call-update) | async-done | bytes 1835024 | tf_op jit(solution)/shard_map/all_gather | solution.py:89
  99.0 11.9 %convolution_bitcast_fusion = f32[1024,2304]{0,1:T(8,128)} fusion(bf16[1024,896]{1,0:T(8,128)(2,1)} %all-gather.3.cloned.1.call-done, bf16[896,576]{0,1:T(8,128)(2,1)S(1)} %get-tuple-element.18, bf16[896,576]{0,1:T(8,128)(2,1)} %get-tuple-element.19, bf16[896,576]{0,1:T(8,128)(2,1)S(1)} %copy-done.6, bf16[896,576]{0,1:T(8,128)(2,1)S(1)} %copy-done.7), kind=kOutput, calls=%fused_computation | convolution fusion | flops 4244373504 | bytes 15400960 | tf_op jit(solution)/shard_map/dot_general | solution.py:96
  110.9 100.8 %reduce-scatter.5.cloned.1.call-done = f32[128,2304]{0,1:T(8,128)} async-done(((f32[1024,2304]{0,1:T(8,128)}), f32[128,2304]{0,1:T(8,128)}) %reduce-scatter.5.cloned.1.call-update) | async-done | bytes 1179664 | tf_op jit(solution)/shard_map/reduce_scatter | solution.py:97
  213.3 1.7 broadcast_in_dim.8
  215.1 6.0 all-to-all-start
  222.5 2.1 multiply_convert_fusion
  224.7 47.2 %all-to-all-done = bf16[8,128,1152]{2,1,0:T(8,128)(2,1)S(1)} async-done(((bf16[8,128,1152]{2,1,0:T(8,128)(2,1)}), bf16[8,128,1152]{2,1,0:T(8,128)(2,1)S(1)}, u32[]{:S(2)}, u32[]{:S(2)}) %all-to-all-start) | async-done | bytes 2359328 | tf_op jit(solution)/shard_map/all_to_all | solution.py:22
  271.9 7.0 %fusion.8 = f32[1024,896]{1,0:T(8,128)} fusion(bf16[1024,1152]{1,0:T(8,128)(2,1)S(1)} %bitcast.19, bf16[576,896]{1,0:T(8,128)(2,1)} %multiply_convert_fusion, bf16[576,896]{1,0:T(8,128)(2,1)} %neg.24), kind=kOutput, calls=%fused_computation.11 | convolution fusion | flops 2118057984 | bytes 8093696 | tf_op jit(solution)/shard_map/dot_general | solution.py:106
  279.0 47.4 %reduce-scatter.7.cloned.1.call-done = f32[256,896]{1,0:T(8,128)} async-done(((f32[1024,896]{1,0:T(8,128)}), f32[256,896]{1,0:T(8,128)}) %reduce-scatter.7.cloned.1.call-update) | async-done | bytes 917520 | tf_op jit(solution)/shard_map/reduce_scatter | solution.py:32
  326.4 26.6 %reduce-scatter.9.cloned.1.call-done = f32[64,896]{1,0:T(8,128)} async-done(((f32[256,896]{1,0:T(8,128)}), f32[64,896]{1,0:T(8,128)}) %reduce-scatter.9.cloned.1.call-update) | async-done | bytes 229392 | tf_op jit(solution)/shard_map/reduce_scatter | solution.py:32
  353.9 23.4 %reduce-scatter.11.cloned.1.call-done = f32[32,896]{1,0:T(8,128)} async-done(((f32[64,896]{1,0:T(8,128)}), f32[32,896]{1,0:T(8,128)}) %reduce-scatter.11.cloned.1.call-update) | async-done | bytes 114704 | tf_op jit(solution)/shard_map/reduce_scatter | solution.py:32
  377.2 2.2 fusion.15
  379.5 85.6 %all-gather.5.cloned.1.call-done = bf16[1024,896]{1,0:T(8,128)(2,1)} async-done(((bf16[32,896]{1,0:T(8,128)(2,1)}), bf16[1024,896]{1,0:T(8,128)(2,1)}) %all-gather.5.cloned.1.call-update) | async-done | bytes 1835024 | tf_op jit(solution)/shard_map/all_gather | solution.py:117
  465.0 2.9 convolution_bitcast_fusion.1
  468.1 57.4 %all_to_all.15 = f32[8,128,576]{1,2,0:T(8,128)S(1)} all-to-all(f32[8,128,576]{1,2,0:T(8,128)S(1)} %bitcast.18), channel_id=1, replica_groups=mesh['dp_0'=4,'dp_1'=4,'dp_2'=2,'mp_0'=4,'mp_1'=2] {'mp_0','mp_1'}, dimensions={0} | all-to-all | bytes 4718592 | tf_op jit(solution)/shard_map/all_to_all | solution.py:50
  530.0 8.4 %all-to-all-start.2 = ((bf16[8,128,1152]{2,1,0:T(8,128)(2,1)}), bf16[8,128,1152]{2,1,0:T(8,128)(2,1)}, u32[]{:S(2)}, u32[]{:S(2)}) async-start(bf16[8,128,1152]{2,1,0:T(8,128)(2,1)} %broadcast_in_dim.9), calls=%async_computation.6 | async-start | bytes 4718592 | tf_op jit(solution)/shard_map/all_to_all | solution.py:22
  538.4 7.8 %psum.35 = f32[]{:T(128)} all-reduce(f32[]{:T(128)} %get-tuple-element.17), channel_id=1, replica_groups=mesh['dp_0'=4,'dp_1'=4,'dp_2'=2,'mp_0'=4,'mp_1'=2] {'dp_0'}, use_global_device_ids=true, to_apply=%region_5.6 | all-reduce | flops 1 | bytes 8 | tf_op jit(solution)/shard_map/psum | solution.py:38
  546.2 8.5 %psum.36 = f32[]{:T(128)} all-reduce(f32[]{:T(128)} %psum.35), channel_id=1, replica_groups=mesh['dp_0'=4,'dp_1'=4,'dp_2'=2,'mp_0'=4,'mp_1'=2] {'dp_1'}, use_global_device_ids=true, to_apply=%region_6.7 | all-reduce | flops 1 | bytes 8 | tf_op jit(solution)/shard_map/psum | solution.py:38
  554.7 14.7 %psum.37 = f32[]{:T(128)} all-reduce(f32[]{:T(128)} %psum.36), channel_id=1, replica_groups=mesh['dp_0'=4,'dp_1'=4,'dp_2'=2,'mp_0'=4,'mp_1'=2] {'dp_2'}, use_global_device_ids=true, to_apply=%region_7.8 | all-reduce | flops 1 | bytes 8 | tf_op jit(solution)/shard_map/psum | solution.py:38
  569.4 23.5 %psum.38 = f32[]{:T(128)} all-reduce(f32[]{:T(128)} %psum.37), channel_id=1, replica_groups=mesh['dp_0'=4,'dp_1'=4,'dp_2'=2,'mp_0'=4,'mp_1'=2] {'mp_0'}, use_global_device_ids=true, to_apply=%region_8.9 | all-reduce | flops 1 | bytes 8 | tf_op jit(solution)/shard_map/psum | solution.py:38
  592.9 4.9 psum.39
  598.5 4.0 convolution_convert_fusion.1
  602.5 4.9 fusion.7
  (53 shorter events, 13.2 us)
Async XLA Ops:
  7.2 91.8 %all-gather.3.cloned.1.call-start = ((), (), s32[]{:S(2)}) async-start(), calls=%async_computation.7 | async-start | bytes 1892352 | tf_op jit(solution)/shard_map/all_gather | solution.py:89
  7.9 203.8 %reduce-scatter.5.cloned.1.call-start = ((), (), s32[]{:S(2)}) async-start(), calls=%async_computation.8 | async-start | bytes 10616832 | tf_op jit(solution)/shard_map/reduce_scatter | solution.py:97
  10.3 88.7 %copy-start.6 = (bf16[896,576]{0,1:T(8,128)(2,1)S(1)}, bf16[896,576]{0,1:T(8,128)(2,1)}, u32[]{:S(2)}) copy-start(bf16[896,576]{0,1:T(8,128)(2,1)} %param.16) | copy-start | bytes 3096580
  10.3 88.6 %copy-start.7 = (bf16[896,576]{0,1:T(8,128)(2,1)S(1)}, bf16[896,576]{0,1:T(8,128)(2,1)}, u32[]{:S(2)}) copy-start(bf16[896,576]{0,1:T(8,128)(2,1)} %param.15) | copy-start | bytes 3096580
  215.1 6.0 copy-start.8
  215.1 6.1 copy-start
  215.1 56.8 %all-to-all-start = ((bf16[8,128,1152]{2,1,0:T(8,128)(2,1)}), bf16[8,128,1152]{2,1,0:T(8,128)(2,1)S(1)}, u32[]{:S(2)}, u32[]{:S(2)}) async-start(bf16[8,128,1152]{2,1,0:T(8,128)(2,1)} %broadcast_in_dim.8), calls=%async_computation.1 | async-start | bytes 4718592 | tf_op jit(solution)/shard_map/all_to_all | solution.py:22
  221.0 1.2 copy-start.9
  221.0 1.2 copy-start.10
  221.0 105.3 %reduce-scatter.7.cloned.1.call-start = ((), (), s32[]{:S(2)}) async-start(), calls=%async_computation.9 | async-start | bytes 4587520 | tf_op jit(solution)/shard_map/reduce_scatter | solution.py:32
  221.1 1.4 copy-start.4
  271.9 7.0 %copy-start.2 = (bf16[8,128,1152]{2,1,0:T(8,128)(2,1)}, bf16[8,128,1152]{2,1,0:T(8,128)(2,1)S(1)}, u32[]{:S(2)}) copy-start(bf16[8,128,1152]{2,1,0:T(8,128)(2,1)S(1)} %all-to-all-done) | copy-start | bytes 7077892
  278.9 186.2 %copy-start.5 = (bf16[576,896]{1,0:T(8,128)(2,1)S(1)}, bf16[576,896]{1,0:T(8,128)(2,1)}, u32[]{:S(2)}) copy-start(bf16[576,896]{1,0:T(8,128)(2,1)} %multiply_convert_fusion) | copy-start | bytes 3096580
  278.9 74.1 %reduce-scatter.9.cloned.1.call-start = ((), (), s32[]{:S(2)}) async-start(), calls=%async_computation.10 | async-start | bytes 1146880 | tf_op jit(solution)/shard_map/reduce_scatter | solution.py:32
  326.4 50.8 %reduce-scatter.11.cloned.1.call-start = ((), (), s32[]{:S(2)}) async-start(), calls=%async_computation.11 | async-start | bytes 344064 | tf_op jit(solution)/shard_map/reduce_scatter | solution.py:32
  353.1 112.0 %all-gather.5.cloned.1.call-start = ((), (), s32[]{:S(2)}) async-start(), calls=%async_computation.12 | async-start | bytes 1892352 | tf_op jit(solution)/shard_map/all_gather | solution.py:117
  525.6 1.4 copy-start.1
  530.0 68.5 %copy-start.3 = (bf16[8,128,1152]{2,1,0:T(8,128)(2,1)S(1)}, bf16[8,128,1152]{2,1,0:T(8,128)(2,1)}, u32[]{:S(2)}) copy-start(bf16[8,128,1152]{2,1,0:T(8,128)(2,1)} %copy-done.2) | copy-start | bytes 7077892
  530.0 72.5 %all-to-all-start.2 = ((bf16[8,128,1152]{2,1,0:T(8,128)(2,1)}), bf16[8,128,1152]{2,1,0:T(8,128)(2,1)}, u32[]{:S(2)}, u32[]{:S(2)}) async-start(bf16[8,128,1152]{2,1,0:T(8,128)(2,1)} %broadcast_in_dim.9), calls=%async_computation.6 | async-start | bytes 4718592 | tf_op jit(solution)/shard_map/all_to_all | solution.py:22
Sparse Core Ops, SparseCore 0:
  11.4 87.5 all-gather.2
  111.0 100.6 reduce-scatter.4
  279.0 47.2 reduce-scatter.6
  328.8 24.2 reduce-scatter.8
  355.4 21.8 reduce-scatter.10
  381.1 83.9 all-gather.4
where the time goes:
time: 618 us; the launch traced here: 617 us
  waiting for transfers between devices  415 us (67%)
  blocking collectives  117 us (19%)
  matrix products  30.7 us (5%)
  other arithmetic  16 us (3%)
  between operations  16 us (3%)
  starting transfers between devices  14.6 us (2%)
  local copies, waits for them, and re-layouts  7.04 us (1%)
    reduce_scatter x1, waiting for transfers between devices, shards(): lax.psum_scatter(partial_value, MP, scatter_dimension=0, tiled=True)  101 us
    reduce_scatter x3, waiting for transfers between devices, scatter_axes(): nearer = lax.psum_scatter(value, axes[0], scatter_dimension=dim, tiled=True)  97.4 us
    all_gather x1, waiting for transfers between devices, shards(): out_grad = lax.all_gather(local_grad, DP, axis=0, tiled=True)  85.6 us
    all_gather x1, waiting for transfers between devices, shards(): all_tokens = lax.all_gather(tokens, DP, axis=0, tiled=True)  83.8 us
    psum x5, blocking collectives, over_axes(): value = lax.psum(value, axis)  59.4 us
    all_to_all x1, blocking collectives, sent_and_summed(): tiles = lax.all_to_all(split_up(value, dim, count), axis, 0, 0, tiled=True)  57.4 us
    all_to_all x2, waiting for transfers between devices, copy_for_each(): return lax.all_to_all(copies, axis, split_axis=0, concat_axis=0, tiled=True)  47.2 us
    all_to_all x2, starting transfers between devices, copy_for_each(): return lax.all_to_all(copies, axis, split_axis=0, concat_axis=0, tiled=True)  14.4 us
  transfers between devices with their start and end apart: 8, of which 7 were waited for; matrix products, arithmetic and copies ran while one was open for 2% of the time, Pallas kernels for 0%

commit v1 on v0

--- a/solution.py
+++ b/solution.py
@@ -86,7 +86,8 @@
 ):
     own_rows = tokens.shape[0]
     hidden_cols = gate_weight.shape[1]
-    all_tokens = lax.all_gather(tokens, DP, axis=0, tiled=True)
+    repeated = jnp.stack([tokens] * lax.axis_size(DP))
+    all_tokens = jnp.concatenate(lax.all_to_all(repeated, DP, 0, 0), axis=0)
     total_rows = all_tokens.shape[0]
     gate_student = soft_weight(
         gate_weight, gate_round, quant_scale[0], quant_bits[0], quant_zero[0], D

time: 618 us -> 587 us (0.950)
  waiting for transfers between devices: 415 us -> 373 us
  starting transfers between devices: 14.6 us -> 26.7 us
    all_gather x1 -> x0, waiting for transfers between devices: 83.8 us -> none  [shards(): all_tokens = lax.all_gather(tokens, DP, axis=0, tiled=True)]
    all_to_all x0 -> x1, waiting for transfers between devices: none -> 44.1 us  [shards(): all_tokens = jnp.concatenate(lax.all_to_all(repeated, DP, 0, 0), axis=0)]
    all_to_all x0 -> x1, starting transfers between devices: none -> 12 us  [shards(): all_tokens = jnp.concatenate(lax.all_to_all(repeated, DP, 0, 0), axis=0)]
where the time goes in v1:
time: 587 us; the launch traced here: 586 us
  waiting for transfers between devices  373 us (64%)
  blocking collectives  117 us (20%)
  matrix products  30.4 us (5%)
  starting transfers between devices  26.7 us (5%)
  between operations  15.7 us (3%)
  other arithmetic  13.8 us (2%)
  local copies, waits for them, and re-layouts  9.25 us (2%)
    reduce_scatter x1, waiting for transfers between devices, shards(): lax.psum_scatter(partial_value, MP, scatter_dimension=0, tiled=True)  98.8 us
    reduce_scatter x3, waiting for transfers between devices, scatter_axes(): nearer = lax.psum_scatter(value, axes[0], scatter_dimension=dim, tiled=True)  97.3 us
    all_gather x1, waiting for transfers between devices, shards(): out_grad = lax.all_gather(local_grad, DP, axis=0, tiled=True)  85.6 us
    psum x5, blocking collectives, over_axes(): value = lax.psum(value, axis)  59.4 us
    all_to_all x1, blocking collectives, sent_and_summed(): tiles = lax.all_to_all(split_up(value, dim, count), axis, 0, 0, tiled=True)  57.4 us
    all_to_all x2, waiting for transfers between devices, copy_for_each(): return lax.all_to_all(copies, axis, split_axis=0, concat_axis=0, tiled=True)  47.2 us
    all_to_all x1, waiting for transfers between devices, shards(): all_tokens = jnp.concatenate(lax.all_to_all(repeated, DP, 0, 0), axis=0)  44.1 us
    all_to_all x2, starting transfers between devices, copy_for_each(): return lax.all_to_all(copies, axis, split_axis=0, concat_axis=0, tiled=True)  14.4 us
  transfers between devices with their start and end apart: 8, of which 7 were waited for; matrix products, arithmetic and copies ran while one was open for 2% of the time, Pallas kernels for 0%

profile of v1, /device:TPU:65, one launch (start us, length us, event | category | flops | bytes accessed | tf_op | source)
XLA Modules:
  0.0 585.8 jit_solution(4994581305114566087)
XLA Ops:
  7.2 2.2 stack.2
  9.4 12.0 %all-to-all-start = ((bf16[32,32,896]{2,1,0:T(8,128)(2,1)}), bf16[32,32,896]{2,1,0:T(8,128)(2,1)S(1)}, u32[]{:S(2)}, u32[]{:S(2)}) async-start(bf16[32,32,896]{2,1,0:T(8,128)(2,1)} %stack.2), calls=%async_computation | async-start | bytes 3670016 | tf_op jit(solution)/shard_map/all_to_all | solution.py:90
  21.6 4.8 multiply_convert_fusion.1
  26.4 44.1 %all-to-all-done = bf16[32,32,896]{2,1,0:T(8,128)(2,1)S(1)} async-done(((bf16[32,32,896]{2,1,0:T(8,128)(2,1)}), bf16[32,32,896]{2,1,0:T(8,128)(2,1)S(1)}, u32[]{:S(2)}, u32[]{:S(2)}) %all-to-all-start) | async-done | bytes 1835040 | tf_op jit(solution)/shard_map/all_to_all | solution.py:90
  70.5 11.5 %convolution_bitcast_fusion = f32[1024,2304]{0,1:T(8,128)} fusion(bf16[1024,896]{1,0:T(8,128)(2,1)S(1)} %bitcast.22, bf16[896,576]{0,1:T(8,128)(2,1)} %get-tuple-element.18, bf16[896,576]{0,1:T(8,128)(2,1)} %get-tuple-element.19, bf16[896,576]{0,1:T(8,128)(2,1)} %param.16, bf16[896,576]{0,1:T(8,128)(2,1)} %param.15), kind=kOutput, calls=%fused_computation | convolution fusion | flops 4244373504 | bytes 15400960 | tf_op jit(solution)/shard_map/dot_general | solution.py:97
  82.1 98.8 %reduce-scatter.5.cloned.1.call-done = f32[128,2304]{0,1:T(8,128)} async-done(((f32[1024,2304]{0,1:T(8,128)}), f32[128,2304]{0,1:T(8,128)}) %reduce-scatter.5.cloned.1.call-update) | async-done | bytes 1179664 | tf_op jit(solution)/shard_map/reduce_scatter | solution.py:98
  184.3 6.0 %all-to-all-start.1 = ((bf16[8,128,1152]{2,1,0:T(8,128)(2,1)}), bf16[8,128,1152]{2,1,0:T(8,128)(2,1)S(1)}, u32[]{:S(2)}, u32[]{:S(2)}) async-start(bf16[8,128,1152]{2,1,0:T(8,128)(2,1)} %broadcast_in_dim.8), calls=%async_computation.2 | async-start | bytes 4718592 | tf_op jit(solution)/shard_map/all_to_all | solution.py:22
  193.9 47.2 %all-to-all-done.1 = bf16[8,128,1152]{2,1,0:T(8,128)(2,1)S(1)} async-done(((bf16[8,128,1152]{2,1,0:T(8,128)(2,1)}), bf16[8,128,1152]{2,1,0:T(8,128)(2,1)S(1)}, u32[]{:S(2)}, u32[]{:S(2)}) %all-to-all-start.1) | async-done | bytes 2359328 | tf_op jit(solution)/shard_map/all_to_all | solution.py:22
  241.0 7.0 %fusion.8 = f32[1024,896]{1,0:T(8,128)} fusion(bf16[1024,1152]{1,0:T(8,128)(2,1)S(1)} %bitcast.20, bf16[576,896]{1,0:T(8,128)(2,1)} %multiply_convert_fusion, bf16[576,896]{1,0:T(8,128)(2,1)} %neg.24), kind=kOutput, calls=%fused_computation.11 | convolution fusion | flops 2118057984 | bytes 8093696 | tf_op jit(solution)/shard_map/dot_general | solution.py:107
  248.2 47.4 %reduce-scatter.7.cloned.1.call-done = f32[256,896]{1,0:T(8,128)} async-done(((f32[1024,896]{1,0:T(8,128)}), f32[256,896]{1,0:T(8,128)}) %reduce-scatter.7.cloned.1.call-update) | async-done | bytes 917520 | tf_op jit(solution)/shard_map/reduce_scatter | solution.py:32
  295.6 26.8 %reduce-scatter.9.cloned.1.call-done = f32[64,896]{1,0:T(8,128)} async-done(((f32[256,896]{1,0:T(8,128)}), f32[64,896]{1,0:T(8,128)}) %reduce-scatter.9.cloned.1.call-update) | async-done | bytes 229392 | tf_op jit(solution)/shard_map/reduce_scatter | solution.py:32
  323.4 23.2 %reduce-scatter.11.cloned.1.call-done = f32[32,896]{1,0:T(8,128)} async-done(((f32[64,896]{1,0:T(8,128)}), f32[32,896]{1,0:T(8,128)}) %reduce-scatter.11.cloned.1.call-update) | async-done | bytes 114704 | tf_op jit(solution)/shard_map/reduce_scatter | solution.py:32
  346.6 2.2 fusion.15
  348.8 85.6 %all-gather.2.cloned.1.call-done = bf16[1024,896]{1,0:T(8,128)(2,1)} async-done(((bf16[32,896]{1,0:T(8,128)(2,1)}), bf16[1024,896]{1,0:T(8,128)(2,1)}) %all-gather.2.cloned.1.call-update) | async-done | bytes 1835024 | tf_op jit(solution)/shard_map/all_gather | solution.py:118
  434.3 2.9 convolution_bitcast_fusion.1
  437.4 57.4 %all_to_all.20 = f32[8,128,576]{1,2,0:T(8,128)S(1)} all-to-all(f32[8,128,576]{1,2,0:T(8,128)S(1)} %bitcast.19), channel_id=1, replica_groups=mesh['dp_0'=4,'dp_1'=4,'dp_2'=2,'mp_0'=4,'mp_1'=2] {'mp_0','mp_1'}, dimensions={0} | all-to-all | bytes 4718592 | tf_op jit(solution)/shard_map/all_to_all | solution.py:50
  499.3 8.4 %all-to-all-start.3 = ((bf16[8,128,1152]{2,1,0:T(8,128)(2,1)}), bf16[8,128,1152]{2,1,0:T(8,128)(2,1)}, u32[]{:S(2)}, u32[]{:S(2)}) async-start(bf16[8,128,1152]{2,1,0:T(8,128)(2,1)} %broadcast_in_dim.9), calls=%async_computation.7 | async-start | bytes 4718592 | tf_op jit(solution)/shard_map/all_to_all | solution.py:22
  507.7 7.7 %psum.35 = f32[]{:T(128)} all-reduce(f32[]{:T(128)} %get-tuple-element.17), channel_id=1, replica_groups=mesh['dp_0'=4,'dp_1'=4,'dp_2'=2,'mp_0'=4,'mp_1'=2] {'dp_0'}, use_global_device_ids=true, to_apply=%region_5.6 | all-reduce | flops 1 | bytes 8 | tf_op jit(solution)/shard_map/psum | solution.py:38
  515.3 8.5 %psum.36 = f32[]{:T(128)} all-reduce(f32[]{:T(128)} %psum.35), channel_id=1, replica_groups=mesh['dp_0'=4,'dp_1'=4,'dp_2'=2,'mp_0'=4,'mp_1'=2] {'dp_1'}, use_global_device_ids=true, to_apply=%region_6.7 | all-reduce | flops 1 | bytes 8 | tf_op jit(solution)/shard_map/psum | solution.py:38
  523.8 14.9 %psum.37 = f32[]{:T(128)} all-reduce(f32[]{:T(128)} %psum.36), channel_id=1, replica_groups=mesh['dp_0'=4,'dp_1'=4,'dp_2'=2,'mp_0'=4,'mp_1'=2] {'dp_2'}, use_global_device_ids=true, to_apply=%region_7.8 | all-reduce | flops 1 | bytes 8 | tf_op jit(solution)/shard_map/psum | solution.py:38
  538.7 23.5 %psum.38 = f32[]{:T(128)} all-reduce(f32[]{:T(128)} %psum.37), channel_id=1, replica_groups=mesh['dp_0'=4,'dp_1'=4,'dp_2'=2,'mp_0'=4,'mp_1'=2] {'mp_0'}, use_global_device_ids=true, to_apply=%region_8.9 | all-reduce | flops 1 | bytes 8 | tf_op jit(solution)/shard_map/psum | solution.py:38
  562.2 4.9 psum.39
  567.8 4.0 convolution_convert_fusion.1
  571.8 4.9 fusion.7
  (59 shorter events, 14.3 us)
Async XLA Ops:
  9.4 12.1 %copy-start.8 = (s32[2,576]{1,0:T(2,128)S(1)}, s32[2,576]{1,0:T(2,128)}, u32[]{:S(2)}) copy-start(s32[2,576]{1,0:T(2,128)} %param.23) | copy-start | bytes 13828
  9.4 12.1 %copy-start.9 = (f32[2,576]{1,0:T(2,128)S(1)}, f32[2,576]{1,0:T(2,128)}, u32[]{:S(2)}) copy-start(f32[2,576]{1,0:T(2,128)} %param.21) | copy-start | bytes 13828
  9.4 12.2 %copy-start.10 = (s32[2,576]{1,0:T(2,128)S(1)}, s32[2,576]{1,0:T(2,128)}, u32[]{:S(2)}) copy-start(s32[2,576]{1,0:T(2,128)} %param.22) | copy-start | bytes 13828
  9.4 12.2 %copy-start.7 = (bf16[896,576]{0,1:T(8,128)(2,1)S(1)}, bf16[896,576]{0,1:T(8,128)(2,1)}, u32[]{:S(2)}) copy-start(bf16[896,576]{0,1:T(8,128)(2,1)} %param.19) | copy-start | bytes 3096580
  9.4 61.1 %all-to-all-start = ((bf16[32,32,896]{2,1,0:T(8,128)(2,1)}), bf16[32,32,896]{2,1,0:T(8,128)(2,1)S(1)}, u32[]{:S(2)}, u32[]{:S(2)}) async-start(bf16[32,32,896]{2,1,0:T(8,128)(2,1)} %stack.2), calls=%async_computation | async-start | bytes 3670016 | tf_op jit(solution)/shard_map/all_to_all | solution.py:90
  21.4 159.5 %reduce-scatter.5.cloned.1.call-start = ((), (), s32[]{:S(2)}) async-start(), calls=%async_computation.8 | async-start | bytes 10616832 | tf_op jit(solution)/shard_map/reduce_scatter | solution.py:98
  70.5 11.5 %copy-start.4 = (bf16[32,32,896]{2,1,0:T(8,128)(2,1)}, bf16[32,32,896]{2,1,0:T(8,128)(2,1)S(1)}, u32[]{:S(2)}) copy-start(bf16[32,32,896]{2,1,0:T(8,128)(2,1)S(1)} %all-to-all-done) | copy-start | bytes 5505028
  184.3 6.0 %copy-start.11 = (s32[896]{0:T(1024)S(1)}, s32[896]{0:T(1024)}, u32[]{:S(2)}) copy-start(s32[896]{0:T(1024)} %param.26) | copy-start | bytes 10756
  184.3 6.1 %copy-start = (bf16[576,896]{1,0:T(8,128)(2,1)S(1)}, bf16[576,896]{1,0:T(8,128)(2,1)}, u32[]{:S(2)}) copy-start(bf16[576,896]{1,0:T(8,128)(2,1)} %param.17) | copy-start | bytes 3096580
  184.3 56.8 %all-to-all-start.1 = ((bf16[8,128,1152]{2,1,0:T(8,128)(2,1)}), bf16[8,128,1152]{2,1,0:T(8,128)(2,1)S(1)}, u32[]{:S(2)}, u32[]{:S(2)}) async-start(bf16[8,128,1152]{2,1,0:T(8,128)(2,1)} %broadcast_in_dim.8), calls=%async_computation.2 | async-start | bytes 4718592 | tf_op jit(solution)/shard_map/all_to_all | solution.py:22
  190.2 1.2 copy-start.12
  190.2 1.2 copy-start.13
  190.2 105.3 %reduce-scatter.7.cloned.1.call-start = ((), (), s32[]{:S(2)}) async-start(), calls=%async_computation.9 | async-start | bytes 4587520 | tf_op jit(solution)/shard_map/reduce_scatter | solution.py:32
  190.3 1.4 copy-start.5
  241.0 7.0 %copy-start.2 = (bf16[8,128,1152]{2,1,0:T(8,128)(2,1)}, bf16[8,128,1152]{2,1,0:T(8,128)(2,1)S(1)}, u32[]{:S(2)}) copy-start(bf16[8,128,1152]{2,1,0:T(8,128)(2,1)S(1)} %all-to-all-done.1) | copy-start | bytes 7077892
  248.1 186.3 %copy-start.6 = (bf16[576,896]{1,0:T(8,128)(2,1)S(1)}, bf16[576,896]{1,0:T(8,128)(2,1)}, u32[]{:S(2)}) copy-start(bf16[576,896]{1,0:T(8,128)(2,1)} %multiply_convert_fusion) | copy-start | bytes 3096580
  248.1 74.3 %reduce-scatter.9.cloned.1.call-start = ((), (), s32[]{:S(2)}) async-start(), calls=%async_computation.10 | async-start | bytes 1146880 | tf_op jit(solution)/shard_map/reduce_scatter | solution.py:32
  295.6 51.0 %reduce-scatter.11.cloned.1.call-start = ((), (), s32[]{:S(2)}) async-start(), calls=%async_computation.11 | async-start | bytes 344064 | tf_op jit(solution)/shard_map/reduce_scatter | solution.py:32
  322.4 111.9 %all-gather.2.cloned.1.call-start = ((), (), s32[]{:S(2)}) async-start(), calls=%async_computation.12 | async-start | bytes 1892352 | tf_op jit(solution)/shard_map/all_gather | solution.py:118
  494.9 1.4 copy-start.1
  499.3 68.5 %copy-start.3 = (bf16[8,128,1152]{2,1,0:T(8,128)(2,1)S(1)}, bf16[8,128,1152]{2,1,0:T(8,128)(2,1)}, u32[]{:S(2)}) copy-start(bf16[8,128,1152]{2,1,0:T(8,128)(2,1)} %copy-done.2) | copy-start | bytes 7077892
  499.3 72.5 %all-to-all-start.3 = ((bf16[8,128,1152]{2,1,0:T(8,128)(2,1)}), bf16[8,128,1152]{2,1,0:T(8,128)(2,1)}, u32[]{:S(2)}, u32[]{:S(2)}) async-start(bf16[8,128,1152]{2,1,0:T(8,128)(2,1)} %broadcast_in_dim.9), calls=%async_computation.7 | async-start | bytes 4718592 | tf_op jit(solution)/shard_map/all_to_all | solution.py:22
Sparse Core Ops, SparseCore 0:
  82.2 98.6 reduce-scatter.4
  248.2 47.2 reduce-scatter.6
  298.1 24.2 reduce-scatter.8
  324.7 21.7 reduce-scatter.10
  350.4 83.9 all-gather.1
